TPU v7x, 32 devices: a whole 2x2x4 slice. The times are simulated.
32 devices in a mesh: seq: 8 (over z, core), grp: 4 (over y, x).
Axes of the slice: x: 2, y: 2, z: 4, core: 2. Of those that a mesh axis runs over, the one named last changes fastest.
Arguments:
- tokens: bfloat16 [16384, 1536], P(('seq', 'grp')), may hold values from -6 to 6
- w_query: bfloat16 [1536, 768], replicated, may hold values from -0.15625 to 0.15625
- w_key: bfloat16 [1536, 768], replicated, may hold values from -0.15625 to 0.15625
- w_value: bfloat16 [1536, 768], replicated, may hold values from -0.15625 to 0.15625
- w_output: bfloat16 [768, 1536], replicated, may hold values from -0.21875 to 0.21875
- level_weights: float32 [9, 6], replicated, may hold values from 0.05 to 0.5
Outputs:
- mixed: bfloat16 [16384, 1536], P(('seq', 'grp'))
All inputs are finite; a program needn't handle non-finite values.
Results may differ from a plain program's by a relative error of at most 0.013.
Values may be sent and summed in bfloat16 or wider, within the bound.
A program may use at most 128 MiB of HBM per device.

v0:
```python
import jax
import jax.numpy as jnp
from jax import lax
from jax.sharding import PartitionSpec as P


def partner_2(value, axis, distance):
    mask = 2**distance
    pairs = [(source, source ^ mask) for source in range(lax.axis_size(axis))]
    return lax.ppermute(value, axis, pairs)


def unit_heads(matrix):
    return (matrix * lax.rsqrt(jnp.sum(matrix * matrix, -1, keepdims=True) + 1e-06)).astype(
        jnp.bfloat16
    )


def sibling_sum(stack, position, level):
    index = jnp.maximum((position >> level) - 1, 0)
    present = (position >> level & 1).astype(jnp.float32)
    return present * lax.dynamic_index_in_dim(stack, index, 0, keepdims=False)


def per_device(tokens, w_query, w_key, w_value, w_output, level_weights):
    rows = tokens.shape[0]
    heads = level_weights.shape[1]
    width = w_query.shape[1] // heads

    def project(weight):
        return jnp.dot(tokens, weight, preferred_element_type=jnp.float32).reshape(
            rows, heads, width
        )

    query = unit_heads(project(w_query))
    keys = unit_heads(project(w_key))
    values = project(w_value).astype(jnp.bfloat16)
    own_state = jnp.einsum("thd,the->hde", keys, values, preferred_element_type=jnp.float32)
    members = lax.axis_size("grp")
    groups = lax.axis_size("seq")
    member = lax.axis_index("grp")
    group = lax.axis_index("seq")
    member_bits = members.bit_length() - 1
    group_bits = groups.bit_length() - 1

    def factor(level):
        return (level_weights[level + 1] * 2.0 ** (-0.5 * level))[:, None, None]

    combined = jnp.zeros((heads, width, width), jnp.float32)
    stack = lax.all_gather(own_state[None].astype(jnp.bfloat16), "grp", axis=0, tiled=True).astype(
        jnp.float32
    )
    for level in range(member_bits):
        grouped = stack.reshape(members >> level, 1 << level, heads, width, width).sum(1)
        combined = combined + factor(level) * sibling_sum(grouped, member, level)
    run_total = jnp.sum(stack, 0)
    block_total = run_total
    for level in range(group_bits):
        partner = partner_2(block_total.astype(jnp.bfloat16), "seq", level).astype(
            block_total.dtype
        )
        present = (group >> level & 1).astype(jnp.float32)
        combined = combined + present * factor(member_bits + level) * partner
        block_total = block_total + partner
    combined = combined.astype(jnp.bfloat16)
    causal = lax.broadcasted_iota(jnp.int32, (rows, rows), 0) >= lax.broadcasted_iota(
        jnp.int32, (rows, rows), 1
    )
    scores = jnp.einsum("thd,shd->hts", query, keys, preferred_element_type=jnp.float32)
    weights = (jnp.where(causal[None], scores, 0.0) * level_weights[0][:, None, None]).astype(
        jnp.bfloat16
    )
    inside = jnp.einsum("hts,she->the", weights, values, preferred_element_type=jnp.float32)
    earlier = jnp.einsum("thd,hde->the", query, combined, preferred_element_type=jnp.float32)
    attended = (inside + earlier).astype(jnp.bfloat16).reshape(rows, heads * width)
    return jnp.dot(attended, w_output, preferred_element_type=jnp.float32).astype(jnp.bfloat16)


def solution(mesh):
    placed = (P(("seq", "grp"), None), P(), P(), P(), P(), P())
    return jax.shard_map(
        per_device, mesh=mesh, in_specs=placed, out_specs=P(("seq", "grp"), None), check_vma=False
    )
```

profile of v0, /device:TPU:0, one launch (start us, length us, event | category | flops | bytes accessed | tf_op | source)
XLA Modules:
  0.0 62.1 jit_solution(12298181707420740750)
XLA Ops:
  0.0 4.5 %convolution_convert_fusion.1 = bf16[512,768]{1,0:T(8,128)(2,1)} fusion(bf16[512,1536]{1,0:T(8,128)(2,1)} %param.6, bf16[1536,768]{1,0:T(8,128)(2,1)} %param.9), kind=kOutput, calls=%fused_computation.12 | convolution fusion | flops 1208352768 | bytes 4718592 | tf_op jit(solution)/shard_map/dot_general | solution.py:31
  4.6 1.4 %copy.18 = bf16[512,768]{0,1:T(8,128)(2,1)S(1)} copy(bf16[512,768]{1,0:T(8,128)(2,1)} %convolution_convert_fusion.1) | data formatting | bytes 1572864 | tf_op jit(solution)/shard_map/convert_element_type | solution.py:37
  6.0 3.6 %fusion.24 = f32[512,768]{0,1:T(8,128)S(1)} fusion(bf16[512,1536]{1,0:T(8,128)(2,1)} %param.6, bf16[1536,768]{1,0:T(8,128)(2,1)} %param.8), kind=kOutput, calls=%fused_computation.46 | convolution fusion | flops 1207959552 | bytes 5505024 | tf_op jit(solution)/shard_map/dot_general | solution.py:31
  9.8 0.4 convolution_convert_fusion.2
  10.2 0.5 copy-done.1
  10.7 12.7 %all-gather = bf16[24,128,128]{2,1,0:T(8,128)(2,1)S(1)} all-gather(bf16[6,128,128]{2,1,0:T(8,128)(2,1)S(1)} %convolution_convert_fusion.2), channel_id=2, replica_groups=mesh['seq'=8,'grp'=4] {'grp'}, dimensions={0}, use_global_device_ids=true | all-gather | bytes 983040 | tf_op jit(solution)/shard_map/all_gather | solution.py:50
  23.4 1.3 %convert_element_type.92 = f32[24,128,128]{2,1,0:T(8,128)} convert(bf16[24,128,128]{2,1,0:T(8,128)(2,1)S(1)} %all-gather) | non-fusion elementwise | flops 393216 | bytes 2359296 | tf_op jit(solution)/shard_map/convert_element_type | solution.py:50
  24.7 1.5 %reduce_sum.43 = f32[6,128,128]{2,1,0:T(8,128)S(1)} reduce(f32[4,6,128,128]{3,2,1,0:T(8,128)} %bitcast.30, f32[]{:T(128)} %constant.13.clone.1), dimensions={0}, to_apply=%region_3.4 | reduce | flops 294912 | bytes 1966084 | tf_op jit(solution)/shard_map/reduce_sum | solution.py:56
  26.2 0.7 %convert_element_type.80 = bf16[6,128,128]{2,1,0:T(8,128)(2,1)} convert(f32[6,128,128]{2,1,0:T(8,128)S(1)} %reduce_sum.43) | non-fusion elementwise | flops 98304 | bytes 589824 | tf_op jit(solution)/shard_map/convert_element_type | solution.py:59
  26.9 0.8 %iota_compare_fusion = pred[512,512]{1,0:T(8,128)(4,1)} fusion(), kind=kLoop, calls=%fused_computation.14 | loop fusion | flops 262144 | bytes 262144 | tf_op jit(solution)/shard_map/ge | solution.py:66
  27.7 4.7 %fusion.23 = f32[512,768]{0,1:T(8,128)} fusion(bf16[512,1536]{1,0:T(8,128)(2,1)} %param.6, bf16[1536,768]{1,0:T(8,128)(2,1)} %param.7), kind=kOutput, calls=%fused_computation.45 | convolution fusion | flops 1207959552 | bytes 5505024 | tf_op jit(solution)/shard_map/dot_general | solution.py:31
  32.5 0.8 %slice_reduce_fusion = (f32[6]{0:T(128)}, f32[6]{0:T(128)}, f32[6]{0:T(128)}, f32[6]{0:T(128)}, f32[6]{0:T(128)}, /*index=5*/f32[6]{0:T(128)}) fusion(f32[9,6]{0,1:T(8,128)S(1)} %copy-done.4, f32[]{:T(128)S(6)} %mul.178, f32[]{:T(128)S(6)} %mul.190, f32[]{:T(128)S(6)} %mul.184), kind=kLoop, calls=%fused_computation.41 | loop fusion | flops 24 | bytes 300 | tf_op jit(solution)/shard_map/slice | solution.py:47
  33.3 1.6 %multiply_reduce_fusion.1 = f32[512,6]{0,1:T(8,128)S(1)} fusion(f32[512,6,128]{0,2,1:T(8,128)} %bitcast.36), kind=kLoop, calls=%fused_computation.11 | loop fusion | flops 783360 | bytes 1585152 | tf_op jit(solution)/shard_map/reduce_sum | solution.py:14
  34.9 1.0 %fusion.12 = bf16[6,128,128]{2,1,0:T(8,128)(2,1)S(1)} fusion(f32[6,128,128]{2,1,0:T(8,128)S(1)} %reduce_sum.43, bf16[6,128,128]{2,1,0:T(8,128)(2,1)} %collective-permute-done), kind=kLoop, calls=%fused_computation.27 | loop fusion | flops 294912 | bytes 786432 | tf_op jit(solution)/shard_map/convert_element_type | solution.py:59
  35.9 1.6 %collective-permute-start.1 = (bf16[6,128,128]{2,1,0:T(8,128)(2,1)S(1)}, bf16[6,128,128]{2,1,0:T(8,128)(2,1)S(1)}, u32[]{:S(2)}, u32[]{:S(2)}) collective-permute-start(bf16[6,128,128]{2,1,0:T(8,128)(2,1)S(1)} %fusion.12), channel_id=1, source_target_pairs={{0,8},{4,12},{8,0},{12,4},{16,24},{20,28},{24,16},{28,20},{1,9},{5... | collective-permute-start | bytes 589832 | tf_op jit(solution)/shard_map/ppermute | solution.py:10
  37.5 0.6 add_rsqrt_fusion.1
  38.2 5.1 %collective-permute-done.1 = bf16[6,128,128]{2,1,0:T(8,128)(2,1)S(1)} collective-permute-done((bf16[6,128,128]{2,1,0:T(8,128)(2,1)S(1)}, bf16[6,128,128]{2,1,0:T(8,128)(2,1)S(1)}, u32[]{:S(2)}, u32[]{:S(2)}) %collective-permute-start.1) | collective-permute-done | bytes 196640 | tf_op jit(solution)/shard_map/ppermute | solution.py:10
  43.3 1.7 %fusion.10 = bf16[6,128,128]{2,1,0:T(8,128)(2,1)} fusion(bf16[6,128,128]{2,1,0:T(8,128)(2,1)S(1)} %collective-permute-done.1, f32[6,128,128]{2,1,0:T(8,128)S(1)} %reduce_sum.43, bf16[6,128,128]{2,1,0:T(8,128)(2,1)} %collective-permute-done), kind=kLoop, calls=%fused_computation.23 | loop fusion | flops 491520 | bytes 983040 | tf_op jit(solution)/shard_map/convert_element_type | solution.py:59
  45.0 2.6 %collective-permute-start.2 = (bf16[6,128,128]{2,1,0:T(8,128)(2,1)}, bf16[6,128,128]{2,1,0:T(8,128)(2,1)S(1)}, u32[]{:S(2)}, u32[]{:S(2)}) collective-permute-start(bf16[6,128,128]{2,1,0:T(8,128)(2,1)} %fusion.10), channel_id=1, source_target_pairs={{0,16},{4,20},{8,24},{12,28},{16,0},{20,4},{24,8},{28,12},{1,17},{... | collective-permute-start | bytes 589832 | tf_op jit(solution)/shard_map/ppermute | solution.py:10
  47.6 5.3 %fusion = f32[6,128,512]{2,1,0:T(8,128)} fusion(bf16[512,6,128]{0,2,1:T(8,128)(2,1)S(1)} %bitcast.41, f32[6]{0:T(128)} %get-tuple-element.8, pred[512,512]{1,0:T(8,128)(4,1)} %iota_compare_fusion, f32[512,6,128]{0,2,1:T(8,128)} %bitcast.37, f32[512,6]{0,1:T(8,128)} %add_rsqrt_fusion.1, f32[512,6,128]{0,2,1:T(8,128)} %bitcast.35, f32[512,6]{0,1:T(8,128)S(1)} %copy-done.6), kind=kOutput, calls=%fused_computation.1 | convolution fusion | flops 811597824 | bytes 5791768 | tf_op jit(solution)/shard_map/hts,she->the/dot_general | solution.py:73
  53.0 1.6 %reduce_sum.42 = f32[2,6,128,128]{3,2,1,0:T(8,128)S(1)} reduce(f32[2,2,6,128,128]{4,3,2,1,0:T(8,128)} %bitcast.31, f32[]{:T(128)} %constant.13.clone.1), dimensions={1}, to_apply=%region_2.0 | reduce | flops 196608 | bytes 2359300 | tf_op jit(solution)/shard_map/reduce_sum | solution.py:54
  54.6 2.2 %collective-permute-done.2 = bf16[6,128,128]{2,1,0:T(8,128)(2,1)S(1)} collective-permute-done((bf16[6,128,128]{2,1,0:T(8,128)(2,1)}, bf16[6,128,128]{2,1,0:T(8,128)(2,1)S(1)}, u32[]{:S(2)}, u32[]{:S(2)}) %collective-permute-start.2) | collective-permute-done | bytes 196640 | tf_op jit(solution)/shard_map/ppermute | solution.py:10
  56.8 2.7 %add_convert_fusion = bf16[6,128,512]{2,1,0:T(8,128)(2,1)S(1)} fusion(f32[6,128,512]{2,1,0:T(8,128)} %fusion, f32[512,6,128]{0,2,1:T(8,128)} %bitcast.38, f32[512,6]{0,1:T(8,128)S(1)} %copy-done.7, bf16[6,128,128]{2,1,0:T(8,128)(2,1)} %collective-permute-done, bf16[6,128,128]{2,1,0:T(8,128)(2,1)S(1)} %copy-done.3, ...), kind=kOutput, calls=%fused_computation.7 | convolution fusion | flops 103710720 | bytes 5327376 | tf_op jit(solution)/shard_map/thd,hde->the/dot_general | solution.py:74
  59.5 2.6 %convolution_convert_fusion = bf16[512,1536]{1,0:T(8,128)(2,1)} fusion(bf16[512,768]{0,1:T(8,128)(2,1)S(1)} %bitcast.39, bf16[768,1536]{1,0:T(8,128)(2,1)S(1)} %copy-done), kind=kOutput, calls=%fused_computation.6 | convolution fusion | flops 1208745984 | bytes 4718592 | tf_op jit(solution)/shard_map/dot_general | solution.py:76
  (19 shorter events, 0.2 us)
Async XLA Ops:
  0.0 59.5 %copy-start = (bf16[768,1536]{1,0:T(8,128)(2,1)S(1)}, bf16[768,1536]{1,0:T(8,128)(2,1)}, u32[]{:S(2)}) copy-start(bf16[768,1536]{1,0:T(8,128)(2,1)} %param.10) | copy-start | bytes 7077892
  9.5 1.1 %copy-start.1 = (f32[512,768]{0,1:T(8,128)}, f32[512,768]{0,1:T(8,128)S(1)}, u32[]{:S(2)}) copy-start(f32[512,768]{0,1:T(8,128)S(1)} %fusion.24) | copy-start | bytes 4718596
  9.8 13.6 %copy-start.5 = (f32[512,6]{0,1:T(8,128)}, f32[512,6]{0,1:T(8,128)S(1)}, u32[]{:S(2)}) copy-start(f32[512,6]{0,1:T(8,128)S(1)} %add_rsqrt_fusion) | copy-start | bytes 36868
  26.9 8.0 %collective-permute-start = (bf16[6,128,128]{2,1,0:T(8,128)(2,1)}, bf16[6,128,128]{2,1,0:T(8,128)(2,1)}, u32[]{:S(2)}, u32[]{:S(2)}) collective-permute-start(bf16[6,128,128]{2,1,0:T(8,128)(2,1)} %convert_element_type.80), channel_id=1, source_target_pairs={{0,4},{4,0},{8,12},{12,8},{16,20},{20,16},{24,28},{28,24},{1,5},{5... | collective-permute-start | bytes 589832 | tf_op jit(solution)/shard_map/ppermute | solution.py:10
  27.7 4.7 %copy-start.4 = (f32[9,6]{0,1:T(8,128)S(1)}, f32[9,6]{0,1:T(8,128)}, u32[]{:S(2)}) copy-start(f32[9,6]{0,1:T(8,128)} %param.11) | copy-start | bytes 652
  33.3 14.3 %copy-start.6 = (f32[512,6]{0,1:T(8,128)S(1)}, f32[512,6]{0,1:T(8,128)}, u32[]{:S(2)}) copy-start(f32[512,6]{0,1:T(8,128)} %copy-done.5) | copy-start | bytes 36868
  35.9 7.4 %collective-permute-start.1 = (bf16[6,128,128]{2,1,0:T(8,128)(2,1)S(1)}, bf16[6,128,128]{2,1,0:T(8,128)(2,1)S(1)}, u32[]{:S(2)}, u32[]{:S(2)}) collective-permute-start(bf16[6,128,128]{2,1,0:T(8,128)(2,1)S(1)} %fusion.12), channel_id=1, source_target_pairs={{0,8},{4,12},{8,0},{12,4},{16,24},{20,28},{24,16},{28,20},{1,9},{5... | collective-permute-start | bytes 589832 | tf_op jit(solution)/shard_map/ppermute | solution.py:10
  43.3 1.7 %copy-start.2 = (bf16[6,128,128]{2,1,0:T(8,128)(2,1)}, bf16[6,128,128]{2,1,0:T(8,128)(2,1)S(1)}, u32[]{:S(2)}) copy-start(bf16[6,128,128]{2,1,0:T(8,128)(2,1)S(1)} %collective-permute-done.1) | copy-start | bytes 589828
  45.0 11.8 %collective-permute-start.2 = (bf16[6,128,128]{2,1,0:T(8,128)(2,1)}, bf16[6,128,128]{2,1,0:T(8,128)(2,1)S(1)}, u32[]{:S(2)}, u32[]{:S(2)}) collective-permute-start(bf16[6,128,128]{2,1,0:T(8,128)(2,1)} %fusion.10), channel_id=1, source_target_pairs={{0,16},{4,20},{8,24},{12,28},{16,0},{20,4},{24,8},{28,12},{1,17},{... | collective-permute-start | bytes 589832 | tf_op jit(solution)/shard_map/ppermute | solution.py:10
  53.0 3.8 %copy-start.3 = (bf16[6,128,128]{2,1,0:T(8,128)(2,1)S(1)}, bf16[6,128,128]{2,1,0:T(8,128)(2,1)}, u32[]{:S(2)}) copy-start(bf16[6,128,128]{2,1,0:T(8,128)(2,1)} %copy-done.2) | copy-start | bytes 589828
  53.0 3.8 %copy-start.7 = (f32[512,6]{0,1:T(8,128)S(1)}, f32[512,6]{0,1:T(8,128)}, u32[]{:S(2)}) copy-start(f32[512,6]{0,1:T(8,128)} %add_rsqrt_fusion.1) | copy-start | bytes 36868
where the time goes:
time: 62.4 us; the launch traced here: 62.1 us
  matrix products  23.8 us (38%)
  blocking collectives  12.7 us (20%)
  other arithmetic  12 us (19%)
  waiting for transfers between devices  7.32 us (12%)
  starting transfers between devices  4.23 us (7%)
  local copies, waits for them, and re-layouts  1.95 us (3%)
    dot_general x3, matrix products, project(): jnp.dot(tokens, weight, preferred_element_type=jnp.float32)  12.8 us
    all_gather x1, blocking collectives, per_device(): lax.all_gather(own_state[None].astype(jnp.bfloat16), 'grp', axis=0, tiled...  12.7 us
    ppermute x3, waiting for transfers between devices, partner_2(): return lax.ppermute(value, axis, pairs)  7.32 us
    dot_general x1, matrix products, per_device(): jnp.einsum('hts,she->the', weights, values, preferred_element_type=jnp.fl...  5.34 us
    ppermute x3, starting transfers between devices, partner_2(): return lax.ppermute(value, axis, pairs)  4.23 us
    convert_element_type x3, other arithmetic, per_device(): block_total.astype(jnp.bfloat16)  3.42 us
    dot_general x1, matrix products, per_device(): jnp.einsum('thd,hde->the', query, combined, preferred_element_type=jnp.fl...  2.68 us
    dot_general x1, matrix products, per_device(): jnp.dot(attended, w_output, preferred_element_type=jnp.float32)  2.56 us
  transfers between devices with their start and end apart: 3, of which 2 were waited for; matrix products, arithmetic and copies ran while one was open for 25% of the time, Pallas kernels for 0%

commit v1 on v0

v1 whole, which is shorter than its diff:
```python
import functools

import jax
import jax.numpy as jnp
from jax import lax
from jax.experimental import pallas as pl
from jax.experimental.pallas import tpu as pltpu
from jax.sharding import PartitionSpec as P

F32 = jnp.float32
BF16 = jnp.bfloat16
MESH = pl.DeviceIdType.MESH
PAIR = 2


def dot(a, b, dims=((1,), (0,))):
    return lax.dot_general(a, b, (dims, ((), ())), preferred_element_type=F32)


def layer(
    members,
    planes,
    heads,
    tok_hbm,
    wq_hbm,
    wk_hbm,
    wv_hbm,
    wo_hbm,
    lw,
    out_hbm,
    tok,
    wq,
    wk,
    wv,
    wo,
    query,
    keys,
    values,
    inside,
    lower,
    shards,
    gathered,
    total,
    arrived,
    local,
    above,
    mine,
    combined,
    result,
    load_sem,
    out_sem,
    a_send,
    a_recv,
    b_send,
    b_recv,
    c_send,
    c_recv,
):
    rows = tok.shape[0]
    width = keys.shape[1] // heads
    chunks = heads // PAIR
    span = PAIR * width
    plane = 2 * members
    shard = shards.shape[2]
    plane_bits = plane.bit_length() - 1
    z_bits = planes.bit_length() - 1
    half = rows // 2

    seq = lax.axis_index("seq")
    grp = lax.axis_index("grp")
    z = lax.div(seq, 2)
    q = lax.rem(seq, 2) * members + grp

    def in_plane(index):
        return (z * 2 + lax.div(index, members), lax.rem(index, members))

    def up(distance):
        return (seq + 2 * distance, grp)

    barrier = pltpu.get_barrier_semaphore()
    for d in range(1, plane):
        pl.semaphore_signal(
            barrier, inc=1, device_id=in_plane(lax.rem(q + d, plane)), device_id_type=MESH
        )
    for d in range(1, planes):
        pl.semaphore_signal(
            barrier,
            inc=1,
            device_id=(lax.rem(z + d, planes) * 2 + lax.rem(seq, 2), grp),
            device_id_type=MESH,
        )

    loads = {}

    def load(name, source, target):
        loads[name] = pltpu.make_async_copy(source, target, load_sem.at[len(loads)])
        loads[name].start()

    def load_chunk(name, source, target, c):
        load((name, c), source.at[:, pl.ds(c * span, span)], target.at[c])

    load("tok0", tok_hbm.at[pl.ds(0, half)], tok.at[pl.ds(0, half)])
    load_chunk("k", wk_hbm, wk, 0)
    load("tok1", tok_hbm.at[pl.ds(half, half)], tok.at[pl.ds(half, half)])
    load_chunk("v", wv_hbm, wv, 0)
    for c in range(1, chunks):
        load_chunk("k", wk_hbm, wk, c)
        load_chunk("v", wv_hbm, wv, c)
    for c in range(chunks):
        load_chunk("q", wq_hbm, wq, c)
    load("o", wo_hbm, wo)

    def unit(block):
        parts = []
        for i in range(PAIR):
            head = block[:, i * width : (i + 1) * width]
            norm = lax.rsqrt(jnp.sum(head * head, -1, keepdims=True) + 1e-06)
            parts.append((head * norm).astype(BF16))
        return jnp.concatenate(parts, 1)

    def cols(c):
        return pl.ds(c * span, span)

    halves = [pl.ds(0, half), pl.ds(half, half)]

    def a_copy(c, slot, source, device):
        return pltpu.make_async_remote_copy(
            src_ref=shards.at[c, slot],
            dst_ref=gathered.at[c, source],
            send_sem=a_send.at[c, slot],
            recv_sem=a_recv.at[c, source],
            device_id=device,
            device_id_type=MESH,
        )

    def b_copy(c, d, device):
        return pltpu.make_async_remote_copy(
            src_ref=total.at[c],
            dst_ref=arrived.at[c, d],
            send_sem=b_send.at[c, d],
            recv_sem=b_recv.at[c, d],
            device_id=device,
            device_id_type=MESH,
        )

    def c_copy(c, slot, source, device):
        return pltpu.make_async_remote_copy(
            src_ref=mine.at[c, slot],
            dst_ref=combined.at[c, source],
            send_sem=c_send.at[c, slot],
            recv_sem=c_recv.at[c, source],
            device_id=device,
            device_id_type=MESH,
        )

    def states(c):
        parts = []
        for i, r in enumerate(halves):
            if c == 0:
                loads[f"tok{i}"].wait()
                if i == 0:
                    loads["k", c].wait()
            elif i == 0:
                loads["k", c].wait()
            keys[r, cols(c)] = unit(dot(tok[r, :], wk[c]))
        loads["v", c].wait()
        for i, r in enumerate(halves):
            v = dot(tok[r, :], wv[c]).astype(BF16)
            values[r, cols(c)] = v
            both = dot(keys[r, cols(c)], v, ((0,), (0,)))
            parts.append(
                [both[i * width : (i + 1) * width, i * width : (i + 1) * width] for i in range(PAIR)]
            )
        whole = []
        for i in range(PAIR):
            lower[c * PAIR + i] = parts[0][i]
            whole.append(parts[0][i] + parts[1][i])
        stacked = jnp.concatenate(whole, 0).reshape(plane, shard, width)
        shards[c] = stacked.astype(BF16)
        if c == 0:
            pl.semaphore_wait(barrier, plane - 1 + planes - 1)
        for d in range(1, plane):
            peer = lax.rem(q + d, plane)
            a_copy(c, peer, q, in_plane(peer)).start()
        gathered[c, q] = shards[c, q]

    def head_of(c):
        return c * PAIR + lax.div(q * shard, width)

    def factor(level, c):
        return lw[level + 1, head_of(c)] * (2.0 ** (-0.5 * level))

    def totals(c):
        for d in range(1, plane):
            peer = lax.rem(q + d, plane)
            a_copy(c, peer, peer, in_plane(peer)).wait_recv()
        sums = [gathered[c, i].astype(F32) for i in range(plane)]
        tree = [sums]
        while len(tree[-1]) > 1:
            last = tree[-1]
            tree.append([last[i] + last[i + 1] for i in range(0, len(last), 2)])
        total[c] = tree[-1][0].astype(BF16)
        for d in range(1, planes):

            @pl.when(z + d < planes)
            def _():
                b_copy(c, d, up(d)).start()

        factors = [factor(level, c) for level in range(plane_bits)]
        for i in range(plane):
            value = jnp.zeros((shard, width), F32)
            for level in range(plane_bits):
                if i >> level & 1:
                    value = value + factors[level] * tree[level][(i >> level) - 1]
            local[c, i] = value

    def combine(c):
        above[c] = jnp.zeros((shard, width), F32)
        for d in range(1, planes):

            @pl.when(z >= d)
            def _():
                level = jnp.int32(0)
                for bit in range(1, z_bits):
                    differ = lax.div(z, 2**bit) != lax.div(z - d, 2**bit)
                    level = level + jnp.where(differ, 1, 0)
                weight = jnp.float32(0.0)
                for bit in range(z_bits):
                    weight = jnp.where(level == bit, factor(plane_bits + bit, c), weight)
                b_copy(c, d, up(d)).wait_recv()
                above[c] = above[c] + weight * arrived[c, d].astype(F32)

        top = above[c]
        for i in range(plane):
            mine[c, i] = (local[c, i] + top).astype(BF16)
        for d in range(1, plane):
            peer = lax.rem(q + d, plane)
            c_copy(c, peer, q, in_plane(peer)).start()
        combined[c, q] = mine[c, q]

    def queries(c):
        loads["q", c].wait()
        for r in halves:
            query[r, cols(c)] = unit(dot(tok[r, :], wq[c]))

    causal = lax.broadcasted_iota(jnp.int32, (half, half), 0) >= lax.broadcasted_iota(
        jnp.int32, (half, half), 1
    )

    def attend(c):
        for i in range(PAIR):
            h = c * PAIR + i
            col = pl.ds(h * width, width)
            for r in halves:
                scores = dot(query[r, col], keys[r, col], ((1,), (1,)))
                weights = (jnp.where(causal, scores, 0.0) * lw[0, h]).astype(BF16)
                inside[r, col] = dot(weights, values[r, col])

    def finish(c):
        for d in range(1, plane):
            peer = lax.rem(q + d, plane)
            c_copy(c, peer, peer, in_plane(peer)).wait_recv()
        state = combined[c].astype(F32).reshape(span, width)
        for i in range(PAIR):
            h = c * PAIR + i
            col = pl.ds(h * width, width)
            first = state[i * width : (i + 1) * width]
            second = first + lw[0, h] * lower[h]
            for r, s in zip(halves, (first, second)):
                earlier = dot(query[r, col], s.astype(BF16))
                keys[r, col] = (inside[r, col] + earlier).astype(BF16)

    for c in range(chunks):
        states(c)
    for c in range(chunks):
        queries(c)
    for c in range(chunks):
        totals(c)
        attend(c)
    for c in range(chunks):
        combine(c)
    loads["o"].wait()
    for c in range(chunks):
        finish(c)
    outs = []
    for i, r in enumerate(halves):
        result[r, :] = dot(keys[r, :], wo[...]).astype(BF16)
        outs.append(pltpu.make_async_copy(result.at[r], out_hbm.at[r], out_sem.at[i]))
        outs[-1].start()

    for c in range(chunks):
        for d in range(1, plane):
            peer = lax.rem(q + d, plane)
            a_copy(c, peer, q, in_plane(peer)).wait_send()
            c_copy(c, peer, q, in_plane(peer)).wait_send()
        for d in range(1, planes):

            @pl.when(z + d < planes)
            def _():
                b_copy(c, d, up(d)).wait_send()

    for copy in outs:
        copy.wait()


def per_device(tokens, w_query, w_key, w_value, w_output, level_weights):
    rows, model = tokens.shape
    inner = w_query.shape[1]
    heads = level_weights.shape[1]
    width = inner // heads
    members = lax.axis_size("grp")
    planes = lax.axis_size("seq") // 2
    plane = 2 * members
    chunks = heads // PAIR
    span = PAIR * width
    shard = span // plane
    anywhere = pl.BlockSpec(memory_space=pl.ANY)
    vmem = pltpu.VMEM
    dma = pltpu.SemaphoreType.DMA
    return pl.pallas_call(
        functools.partial(layer, members, planes, heads),
        out_shape=jax.ShapeDtypeStruct((rows, w_output.shape[1]), BF16),
        in_specs=[anywhere] * 5 + [pl.BlockSpec(memory_space=pltpu.SMEM)],
        out_specs=anywhere,
        scratch_shapes=[
            vmem((rows, model), BF16),
            vmem((chunks, model, span), BF16),
            vmem((chunks, model, span), BF16),
            vmem((chunks, model, span), BF16),
            vmem((inner, w_output.shape[1]), BF16),
            vmem((rows, inner), BF16),
            vmem((rows, inner), BF16),
            vmem((rows, inner), BF16),
            vmem((rows, inner), F32),
            vmem((heads, width, width), F32),
            vmem((chunks, plane, shard, width), BF16),
            vmem((chunks, plane, shard, width), BF16),
            vmem((chunks, shard, width), BF16),
            vmem((chunks, planes, shard, width), BF16),
            vmem((chunks, plane, shard, width), F32),
            vmem((chunks, shard, width), F32),
            vmem((chunks, plane, shard, width), BF16),
            vmem((chunks, plane, shard, width), BF16),
            vmem((rows, w_output.shape[1]), BF16),
            dma((3 + 3 * chunks,)),
            dma((2,)),
            dma((chunks, plane)),
            dma((chunks, plane)),
            dma((chunks, planes)),
            dma((chunks, planes)),
            dma((chunks, plane)),
            dma((chunks, plane)),
        ],
        compiler_params=pltpu.CompilerParams(
            collective_id=0, has_side_effects=True, vmem_limit_bytes=62 * 2**20
        ),
    )(tokens, w_query, w_key, w_value, w_output, level_weights)


def solution(mesh):
    placed = (P(("seq", "grp"), None), P(), P(), P(), P(), P())
    return jax.shard_map(
        per_device, mesh=mesh, in_specs=placed, out_specs=P(("seq", "grp"), None), check_vma=False
    )
```

time: 62.4 us -> 27.5 us (0.44)
  matrix products: 23.8 us -> 0 us
  Pallas kernels: 0 us -> 23.3 us
  blocking collectives: 12.7 us -> 0 us
  other arithmetic: 12 us -> 0 us
  waiting for transfers between devices: 7.32 us -> 0 us
  starting transfers between devices: 4.23 us -> 0 us
  local copies, waits for them, and re-layouts: 1.95 us -> 4.02 us
    dot_general x7 -> x0, matrix products: 23.8 us -> none  [the longest x3 12.8 us: project(): jnp.dot(tokens, weight, preferred_element_type=jnp.float32)]
    pallas_call x0 -> x1, Pallas kernels: none -> 23.3 us  [per_device(): pl.pallas_call(functools.partial(layer, members, planes, heads), out_shap...]
    all_gather x1 -> x0, blocking collectives: 12.7 us -> none  [per_device(): lax.all_gather(own_state[None].astype(jnp.bfloat16), 'grp', axis=0, tiled...]
    ppermute x3 -> x0, waiting for transfers between devices: 7.32 us -> none  [partner_2(): return lax.ppermute(value, axis, pairs)]
    reduce_sum x4 -> x0, other arithmetic: 4.98 us -> none  [the longest x2 1.81 us: unit_heads(): jnp.sum(matrix * matrix, -1, keepdims=True) + 1e-06]
    convert_element_type x4 -> x0, other arithmetic: 4.76 us -> none  [the longest x3 3.42 us: per_device(): block_total.astype(jnp.bfloat16)]
    ppermute x3 -> x0, starting transfers between devices: 4.23 us -> none  [partner_2(): return lax.ppermute(value, axis, pairs)]
    unnamed x16 -> x2, local copies, waits for them, and re-layouts: 0.54 us -> 4.02 us
  transfers between devices with their start and end apart: 3 -> 0, of which waited for: 2 -> 0; matrix products, arithmetic and copies ran while one was open for 25% -> 0% of each run, Pallas kernels for 0% -> 0%
where the time goes in v1:
time: 27.5 us; the launch traced here: 27.3 us
  Pallas kernels  23.3 us (85%)
  local copies, waits for them, and re-layouts  4.02 us (15%)
    pallas_call x1, Pallas kernels, per_device(): pl.pallas_call(functools.partial(layer, members, planes, heads), out_shap...  23.3 us
    unnamed x2, local copies, waits for them, and re-layouts  4.02 us

profile of v1, /device:TPU:0, one launch (start us, length us, event | category | flops | bytes accessed | tf_op | source)
XLA Modules:
  0.0 27.3 jit_solution(15491316821670967020)
XLA Ops:
  0.0 1.4 %copy.7.lw = f32[9,6]{1,0:T(8,128)} copy(f32[9,6]{0,1:T(8,128)} %param.11) | data formatting | bytes 432 | tf_op args[5]
  1.4 23.3 %shard_map.64 = bf16[512,1536]{1,0:T(8,128)(2,1)} custom-call(bf16[512,1536]{1,0:T(8,128)(2,1)} %tok_hbm.1, bf16[1536,768]{1,0:T(8,128)(2,1)} %wq_hbm.1, bf16[1536,768]{1,0:T(8,128)(2,1)} %wk_hbm.1, bf16[1536,768]{1,0:T(8,128)(2,1)} %wv_hbm.1, bf16[768,1536]{1,0:T(8,128)(2,1)} %wo_hbm.1, f32[9,6]{1,0:T(8,128)} %copy.7.lw), custom_call_target="tpu_custom_call" | custom-call | tf_op jit(solution)/shard_map/pallas_call | solution.py:320
  24.6 2.7 %copy.9 = bf16[512,1536]{1,0:T(8,128)(2,1)} copy(bf16[512,1536]{1,0:T(8,128)(2,1)} %shard_map.64) | data formatting | bytes 3145728

commit v2 on v1

--- a/solution.py
+++ b/solution.py
@@ -25,14 +25,12 @@
     wq_hbm,
     wk_hbm,
     wv_hbm,
-    wo_hbm,
     lw,
     out_hbm,
     tok,
     wq,
     wk,
     wv,
-    wo,
     query,
     keys,
     values,
@@ -46,7 +44,6 @@
     above,
     mine,
     combined,
-    result,
     load_sem,
     out_sem,
     a_send,
@@ -108,7 +105,6 @@
         load_chunk("v", wv_hbm, wv, c)
     for c in range(chunks):
         load_chunk("q", wq_hbm, wq, c)
-    load("o", wo_hbm, wo)
 
     def unit(block):
         parts = []
@@ -188,7 +184,7 @@
         return c * PAIR + lax.div(q * shard, width)
 
     def factor(level, c):
-        return lw[level + 1, head_of(c)] * (2.0 ** (-0.5 * level))
+        return lw[head_of(c), level + 1] * (2.0 ** (-0.5 * level))
 
     def totals(c):
         for d in range(1, plane):
@@ -253,7 +249,7 @@
             col = pl.ds(h * width, width)
             for r in halves:
                 scores = dot(query[r, col], keys[r, col], ((1,), (1,)))
-                weights = (jnp.where(causal, scores, 0.0) * lw[0, h]).astype(BF16)
+                weights = (jnp.where(causal, scores, 0.0) * lw[h, 0]).astype(BF16)
                 inside[r, col] = dot(weights, values[r, col])
 
     def finish(c):
@@ -265,7 +261,7 @@
             h = c * PAIR + i
             col = pl.ds(h * width, width)
             first = state[i * width : (i + 1) * width]
-            second = first + lw[0, h] * lower[h]
+            second = first + lw[h, 0] * lower[h]
             for r, s in zip(halves, (first, second)):
                 earlier = dot(query[r, col], s.astype(BF16))
                 keys[r, col] = (inside[r, col] + earlier).astype(BF16)
@@ -279,13 +275,11 @@
         attend(c)
     for c in range(chunks):
         combine(c)
-    loads["o"].wait()
     for c in range(chunks):
         finish(c)
     outs = []
     for i, r in enumerate(halves):
-        result[r, :] = dot(keys[r, :], wo[...]).astype(BF16)
-        outs.append(pltpu.make_async_copy(result.at[r], out_hbm.at[r], out_sem.at[i]))
+        outs.append(pltpu.make_async_copy(keys.at[r], out_hbm.at[r], out_sem.at[i]))
         outs[-1].start()
 
     for c in range(chunks):
@@ -317,17 +311,16 @@
     anywhere = pl.BlockSpec(memory_space=pl.ANY)
     vmem = pltpu.VMEM
     dma = pltpu.SemaphoreType.DMA
-    return pl.pallas_call(
+    attended = pl.pallas_call(
         functools.partial(layer, members, planes, heads),
-        out_shape=jax.ShapeDtypeStruct((rows, w_output.shape[1]), BF16),
-        in_specs=[anywhere] * 5 + [pl.BlockSpec(memory_space=pltpu.SMEM)],
+        out_shape=jax.ShapeDtypeStruct((rows, inner), BF16),
+        in_specs=[anywhere] * 4 + [pl.BlockSpec(memory_space=pltpu.SMEM)],
         out_specs=anywhere,
         scratch_shapes=[
             vmem((rows, model), BF16),
             vmem((chunks, model, span), BF16),
             vmem((chunks, model, span), BF16),
             vmem((chunks, model, span), BF16),
-            vmem((inner, w_output.shape[1]), BF16),
             vmem((rows, inner), BF16),
             vmem((rows, inner), BF16),
             vmem((rows, inner), BF16),
@@ -341,7 +334,6 @@
             vmem((chunks, shard, width), F32),
             vmem((chunks, plane, shard, width), BF16),
             vmem((chunks, plane, shard, width), BF16),
-            vmem((rows, w_output.shape[1]), BF16),
             dma((3 + 3 * chunks,)),
             dma((2,)),
             dma((chunks, plane)),
@@ -352,9 +344,10 @@
             dma((chunks, plane)),
         ],
         compiler_params=pltpu.CompilerParams(
-            collective_id=0, has_side_effects=True, vmem_limit_bytes=62 * 2**20
+            collective_id=0, has_side_effects=True, vmem_limit_bytes=60*2**20
         ),
-    )(tokens, w_query, w_key, w_value, w_output, level_weights)
+    )(tokens, w_query, w_key, w_value, level_weights.T)
+    return dot(attended, w_output).astype(BF16)
 
 
 def solution(mesh):

time: 27.5 us -> 25.9 us (0.942)
  local copies, waits for them, and re-layouts: 4.02 us -> 0.01 us
  matrix products: 0 us -> 3.66 us
  Pallas kernels: 23.3 us -> 22.1 us
    unnamed x2, local copies, waits for them, and re-layouts: 4.02 us -> 0.01 us
    dot_general x0 -> x1, matrix products: none -> 3.66 us  [dot(): return lax.dot_general(a, b, (dims, ((), ())), preferred_element_type=F32)]
    pallas_call x1, Pallas kernels: 23.3 us -> 22.1 us  [per_device(): pl.pallas_call(functools.partial(layer, members, planes, heads), out_shap...]
where the time goes in v2:
time: 25.9 us; the launch traced here: 25.8 us
  Pallas kernels  22.1 us (85%)
  matrix products  3.66 us (14%)
    pallas_call x1, Pallas kernels, per_device(): pl.pallas_call(functools.partial(layer, members, planes, heads), out_shap...  22.1 us
    dot_general x1, matrix products, dot(): return lax.dot_general(a, b, (dims, ((), ())), preferred_element_type=F32)  3.66 us

profile of v2, /device:TPU:0, one launch (start us, length us, event | category | flops | bytes accessed | tf_op | source)
XLA Modules:
  0.0 25.8 jit_solution(13650908684188207942)
XLA Ops:
  0.0 0.0 copy-start
  0.0 22.1 %shard_map.64 = bf16[512,768]{1,0:T(8,128)(2,1)} custom-call(bf16[512,1536]{1,0:T(8,128)(2,1)} %tok_hbm.1, bf16[1536,768]{1,0:T(8,128)(2,1)} %wq_hbm.1, bf16[1536,768]{1,0:T(8,128)(2,1)} %wk_hbm.1, bf16[1536,768]{1,0:T(8,128)(2,1)} %wv_hbm.1, f32[6,9]{1,0:T(8,128)} %bitcast.3), custom_call_target="tpu_custom_call" | custom-call | tf_op jit(solution)/shard_map/pallas_call | solution.py:314
  22.1 0.0 copy-done
  22.1 3.7 %convolution_convert_fusion = bf16[512,1536]{1,0:T(8,128)(2,1)} fusion(bf16[512,768]{1,0:T(8,128)(2,1)} %shard_map.64, bf16[768,1536]{1,0:T(8,128)(2,1)S(1)} %copy-done), kind=kOutput, calls=%fused_computation | convolution fusion | flops 1208745984 | bytes 4718592 | tf_op jit(solution)/shard_map/dot_general | solution.py:17
Async XLA Ops:
  0.0 22.1 %copy-start = (bf16[768,1536]{1,0:T(8,128)(2,1)S(1)}, bf16[768,1536]{1,0:T(8,128)(2,1)}, u32[]{:S(2)}) copy-start(bf16[768,1536]{1,0:T(8,128)(2,1)} %param.10) | copy-start | bytes 7077892
